TPU v7x, 128 devices: a whole 4x4x4 slice. The times are simulated.
128 devices in a mesh: grp: 8 (over x, core), row: 16 (over z, y).
Axes of the slice: x: 4, y: 4, z: 4, core: 2. Of those that a mesh axis runs over, the one named last changes fastest.
Arguments:
- iterate: bfloat16 [64, 1048576], P(None, ('grp', 'row')), may hold values from -6 to 6
- near_tiles: bfloat16 [8192, 128, 128], P(('grp', 'row')), may hold values from -0.125 to 0.125
- near_rows: int32 [8192], P(('grp', 'row')), may hold values from 0 to 63
- near_cols: int32 [8192], P(('grp', 'row')), may hold values from 0 to 63
- near_count: int32 [128], P(('grp', 'row')), may hold values from 32 to 64, as said below
- cross_tiles: bfloat16 [8192, 128, 128], P(('grp', 'row')), may hold values from -0.125 to 0.125
- cross_rows: int32 [8192], P(('grp', 'row')), may hold values from 0 to 63
- cross_cols: int32 [8192], P(('grp', 'row')), may hold values from 0 to 63
- cross_count: int32 [128], P(('grp', 'row')), may hold values from 0 to 64, as said below
Outputs:
- basis: float32 [64, 1048576], P(None, ('grp', 'row'))
- rayleigh: float32 [64, 64], replicated
Inputs may be any that keep to these rules, and one draw needn't show every extreme that they name: `near_count`: slots at or past a device's count hold no part of the matrix. Some device uses all 64 near slots. `cross_count`: the last device's count is 0; some other device uses all 64 cross slots. `near_rows`: positions may repeat; repeated tiles add.
All inputs are finite; a program needn't handle non-finite values.
Results may differ from a plain program's by a relative error of at most 0.003.
Values may be sent and summed in bfloat16 or wider, within the bound.
No kernel may reach another device: no remote copies, remote signals or barrier semaphores. Data moves between devices by JAX's collectives and lax.ppermute only.
A program may use at most 128 MiB of HBM per device.

v0:
```python
import jax
import jax.numpy as jnp
from jax import lax
from jax.sharding import Mesh
from jax.sharding import PartitionSpec as P

EIGS = 64
TILE = 128
BR_DEV = 64
GRP_ROW = ("grp_0", "grp_1", "row_0", "row_1")


def from_behind(array, axis, by):
    devices = lax.axis_size(axis)
    pairs = [(i, i + by) for i in range(devices) if 0 <= i + by < devices]
    return lax.ppermute(array, axis, pairs)


def extended(array, sides, width):
    edges = {}
    for axis, dim in sides:
        devices, length = (lax.axis_size(axis), array.shape[dim])
        up = [(i, (i + 1) % devices) for i in range(devices - 1)]
        last = lax.slice_in_dim(array, length - width, length, axis=dim)
        leading = lax.slice_in_dim(array, 0, width, axis=dim)
        edges[dim] = (
            lax.ppermute(last, axis, up),
            lax.ppermute(leading, axis, [(b, a) for a, b in up]),
        )
    done = []
    for _, dim in sides:
        low, high = edges[dim]
        around = [(width, width) if d in done else (0, 0) for d in range(array.ndim)]
        array = jnp.concatenate([jnp.pad(low, around), array, jnp.pad(high, around)], axis=dim)
        done.append(dim)
    return array


def over_axes(array, axes):
    for axis in axes:
        array = lax.psum(array, axis)
    return array


def tile_terms(blocks, index, tiles, flipped):
    picked = jnp.take(blocks, index, axis=1)
    if flipped:
        return jnp.einsum("ktr,trc->tkc", picked, tiles, preferred_element_type=jnp.float32)
    return jnp.einsum("ktc,trc->tkr", picked, tiles, preferred_element_type=jnp.float32)


def place(terms, index, weight):
    selector = jax.nn.one_hot(index, BR_DEV, dtype=jnp.float32) * weight[:, None]
    placed = jnp.einsum(
        "ts,tkc->ksc",
        selector,
        terms,
        precision=lax.Precision.HIGHEST,
        preferred_element_type=jnp.float32,
    )
    return placed.reshape(EIGS, BR_DEV * TILE)


def shards(
    iterate,
    near_tiles,
    near_rows,
    near_cols,
    near_count,
    cross_tiles,
    cross_rows,
    cross_cols,
    cross_count,
):
    width = BR_DEV * TILE
    near_mask = (jnp.arange(near_tiles.shape[0], dtype=jnp.int32) < near_count[0]).astype(
        jnp.float32
    )
    cross_mask = (jnp.arange(cross_tiles.shape[0], dtype=jnp.int32) < cross_count[0]).astype(
        jnp.float32
    )
    lent_tiles, lent_rows, lent_cols, lent_count = from_behind(
        (cross_tiles, cross_rows, cross_cols, cross_count), GRP_ROW, 1
    )
    lent_mask = (jnp.arange(lent_tiles.shape[0], dtype=jnp.int32) < lent_count[0]).astype(
        jnp.float32
    )

    def apply_s(vector_b):
        blocks = vector_b.reshape(EIGS, BR_DEV, TILE)
        padded = extended(vector_b, ((GRP_ROW, 1),), width)
        behind = padded[:, :width].reshape(EIGS, BR_DEV, TILE)
        ahead = padded[:, 2 * width :].reshape(EIGS, BR_DEV, TILE)
        total = place(tile_terms(blocks, near_cols, near_tiles, False), near_rows, near_mask)
        total = total + place(tile_terms(blocks, near_rows, near_tiles, True), near_cols, near_mask)
        total = total + place(
            tile_terms(ahead, cross_cols, cross_tiles, False), cross_rows, cross_mask
        )
        total = total + place(tile_terms(behind, lent_rows, lent_tiles, True), lent_cols, lent_mask)
        return total

    def mapped(current):
        return (-0.25 * current - apply_s(current.astype(jnp.bfloat16))) / 0.75

    before = iterate.astype(jnp.float32)
    current = mapped(before)
    for step in range(3):
        following = 2.0 * mapped(current) - before
        before, current = (current, following)
    rounded = current.astype(jnp.bfloat16)
    rounded_f = rounded.astype(jnp.float32)
    count_rows = float(width * lax.axis_size(GRP_ROW))
    local_gram = jnp.dot(
        current, current.T, precision=lax.Precision.HIGHEST, preferred_element_type=jnp.float32
    )
    image = rounded_f - apply_s(rounded)
    local_proj = jnp.dot(
        rounded_f, image.T, precision=lax.Precision.HIGHEST, preferred_element_type=jnp.float32
    )
    gram, projected = (over_axes(local_gram, GRP_ROW), over_axes(local_proj, GRP_ROW))
    lower = jnp.linalg.cholesky(gram / count_rows)
    basis = jax.scipy.linalg.solve_triangular(lower, current, lower=True)
    halfway = jax.scipy.linalg.solve_triangular(lower, projected / count_rows, lower=True)
    rayleigh = jax.scipy.linalg.solve_triangular(lower, halfway.T, lower=True)
    return (basis, rayleigh)


def solution(mesh):
    finer = Mesh(mesh.devices.reshape(4, 2, 4, 4), ("grp_0", "grp_1", "row_0", "row_1"))
    in_specs = (
        P(None, GRP_ROW),
        P(GRP_ROW, None, None),
        P(GRP_ROW),
        P(GRP_ROW),
        P(GRP_ROW),
        P(GRP_ROW, None, None),
        P(GRP_ROW),
        P(GRP_ROW),
        P(GRP_ROW),
    )
    out_specs = (P(None, GRP_ROW), P())
    return jax.shard_map(
        shards, mesh=finer, in_specs=in_specs, out_specs=out_specs, check_vma=False
    )
```

profile of v0, /device:TPU:0, one launch (start us, length us, event | category | flops | bytes accessed | tf_op | source)
XLA Modules:
  0.0 438.3 jit_solution(2132862414698501512)
XLA Ops:
  2.1 5.6 %collective-permute-start.1 = (bf16[64,8192]{1,0:T(8,128)(2,1)}, bf16[64,8192]{1,0:T(8,128)(2,1)}, u32[]{:S(2)}, u32[]{:S(2)}) collective-permute-start(bf16[64,8192]{1,0:T(8,128)(2,1)} %param.13), channel_id=1, source_target_pairs={{0,1},{1,2},{2,3},{3,4},{4,5},{5,6},{6,7},{7,8},{8,9},{9,10},{10,1... | collective-permute-start | bytes 3145736 | tf_op jit(solution)/shard_map/ppermute | solution.py:27
  7.7 3.9 collective-permute-start.3
  14.3 4.7 %collective-permute-start.4 = (s32[64]{0:T(128)}, s32[64]{0:T(128)S(1)}, u32[]{:S(2)}, u32[]{:S(2)}) collective-permute-start(s32[64]{0:T(128)} %param.20), channel_id=1, source_target_pairs={{0,1},{1,2},{2,3},{3,4},{4,5},{5,6},{6,7},{7,8},{8,9},{9,10},{10,1... | collective-permute-start | bytes 776 | tf_op jit(solution)/shard_map/ppermute | solution.py:16
  28.8 4.6 %fusion.46 = f32[64,128,64]{1,2,0:T(8,128)} fusion(f32[64,64,128]{2,1,0:T(8,128)S(1)} %fusion.97, f32[64]{0:T(128)S(1)} %compare_convert_fusion.2, s32[64]{0:T(128)S(1)} %copy-done.28), kind=kOutput, calls=%fused_computation.72 | convolution fusion | flops 402661376 | bytes 4194816 | tf_op jit(solution)/shard_map/ts,tkc->ksc/dot_general | solution.py:54
  34.2 4.6 %fusion.44 = f32[64,128,64]{1,2,0:T(8,128)} fusion(f32[64,64,128]{2,1,0:T(8,128)S(1)} %fusion.95, s32[64]{0:T(128)S(1)} %copy-done.29, f32[64]{0:T(128)S(1)} %compare_convert_fusion.2), kind=kOutput, calls=%fused_computation.70 | convolution fusion | flops 402661376 | bytes 4194816 | tf_op jit(solution)/shard_map/ts,tkc->ksc/dot_general | solution.py:54
  38.8 32.6 %collective-permute-done.5 = s32[1]{0:T(128)} collective-permute-done((s32[1]{0:T(128)}, s32[1]{0:T(128)}, u32[]{:S(2)}, u32[]{:S(2)}) %collective-permute-start.5) | collective-permute-done | bytes 36 | tf_op jit(solution)/shard_map/ppermute | solution.py:16
  71.4 6.4 %collective-permute-start.2 = (s32[64]{0:T(128)S(1)}, s32[64]{0:T(128)S(1)}, u32[]{:S(2)}, u32[]{:S(2)}) collective-permute-start(s32[64]{0:T(128)S(1)} %copy-done.30), channel_id=1, source_target_pairs={{0,1},{1,2},{2,3},{3,4},{4,5},{5,6},{6,7},{7,8},{8,9},{9,10},{10,1... | collective-permute-start | bytes 776 | tf_op jit(solution)/shard_map/ppermute | solution.py:16
  85.4 3.5 fusion.93
  88.8 3.3 fusion.42
  95.0 3.8 add_add_fusion.4
  105.1 2.9 gather_fusion.4
  108.0 3.0 gather_fusion.5
  111.0 6.4 %collective-permute-start.7 = (bf16[64,8192]{1,0:T(8,128)(2,1)}, bf16[64,8192]{1,0:T(8,128)(2,1)}, u32[]{:S(2)}, u32[]{:S(2)}) collective-permute-start(bf16[64,8192]{1,0:T(8,128)(2,1)} %multiply_convert_fusion), channel_id=1, source_target_pairs={{0,1},{1,2},{2,3},{3,4},{4,5},{5,6},{6,7},{7,8},{8,9},{9,10},{10,1... | collective-permute-start | bytes 3145736 | tf_op jit(solution)/shard_map/ppermute | solution.py:27
  117.4 2.8 fusion.89
  120.2 4.6 %fusion.38 = f32[64,128,64]{1,2,0:T(8,128)} fusion(f32[64,64,128]{2,1,0:T(8,128)S(1)} %fusion.89, f32[64]{0:T(128)S(1)} %compare_convert_fusion.2, s32[64]{0:T(128)S(1)} %copy-done.28), kind=kOutput, calls=%fused_computation.64 | convolution fusion | flops 402661376 | bytes 4194816 | tf_op jit(solution)/shard_map/ts,tkc->ksc/dot_general | solution.py:54
  125.6 4.7 %fusion.36 = f32[64,128,64]{1,2,0:T(8,128)} fusion(f32[64,64,128]{2,1,0:T(8,128)S(1)} %fusion.87, s32[64]{0:T(128)S(1)} %copy-done.29, f32[64]{0:T(128)S(1)} %compare_convert_fusion.2), kind=kOutput, calls=%fused_computation.62 | convolution fusion | flops 402661376 | bytes 4194816 | tf_op jit(solution)/shard_map/ts,tkc->ksc/dot_general | solution.py:54
  132.9 2.9 gather_fusion.6
  135.7 3.5 fusion.85
  139.2 4.9 %fusion.34 = f32[64,128,64]{1,2,0:T(8,128)} fusion(f32[64,64,128]{2,1,0:T(8,128)S(1)} %fusion.85, f32[64]{0:T(128)S(1)} %compare_convert_fusion.1, s32[64]{0:T(128)S(1)} %copy-done.30), kind=kOutput, calls=%fused_computation.60 | convolution fusion | flops 402661376 | bytes 4194816 | tf_op jit(solution)/shard_map/ts,tkc->ksc/dot_general | solution.py:54
  146.7 2.9 gather_fusion.7
  149.6 2.8 fusion.83
  152.7 5.5 %add_add_fusion.3 = f32[64,128,64]{1,2,0:T(8,128)S(1)} fusion(f32[64,128,64]{1,2,0:T(8,128)} %fusion.34, f32[64,128,64]{1,2,0:T(8,128)S(1)} %copy-done.16, f32[64,128,64]{1,2,0:T(8,128)S(1)} %copy-done.19, f32[64,64,128]{2,1,0:T(8,128)S(1)} %fusion.83, f32[64]{0:T(128)S(1)} %compare_convert_fusion, s32[64]{0:T(128)S(1)} %collective-permute-done.4), kind=kOutput, calls=%fused_computation.78 | convolution fusion | flops 404234240 | bytes 10486272 | tf_op jit(solution)/shard_map/ts,tkc->ksc/dot_general | solution.py:54
  158.3 4.4 %fusion.310 = bf16[64,8192]{1,0:T(8,128)(2,1)} fusion(f32[8,8,64,128]{3,2,1,0:T(8,128)S(1)} %bitcast.311, f32[8,8,64,128]{3,2,1,0:T(8,128)S(1)} %bitcast.308, bf16[64,8192]{1,0:T(8,128)(2,1)S(1)} %copy-done.9), kind=kLoop, calls=%fused_computation.374 | loop fusion | flops 4194304 | bytes 6291456 | tf_op jit(solution)/shard_map/convert_element_type | solution.py:103
  166.5 2.9 gather_fusion.8
  169.4 2.9 gather_fusion.9
  172.4 5.7 %collective-permute-start.9 = (bf16[64,8192]{1,0:T(8,128)(2,1)}, bf16[64,8192]{1,0:T(8,128)(2,1)}, u32[]{:S(2)}, u32[]{:S(2)}) collective-permute-start(bf16[64,8192]{1,0:T(8,128)(2,1)} %fusion.310), channel_id=1, source_target_pairs={{0,1},{1,2},{2,3},{3,4},{4,5},{5,6},{6,7},{7,8},{8,9},{9,10},{10,1... | collective-permute-start | bytes 3145736 | tf_op jit(solution)/shard_map/ppermute | solution.py:27
  178.1 2.8 fusion.81
  180.9 4.7 %fusion.30 = f32[64,128,64]{1,2,0:T(8,128)} fusion(f32[64,64,128]{2,1,0:T(8,128)S(1)} %fusion.81, f32[64]{0:T(128)S(1)} %compare_convert_fusion.2, s32[64]{0:T(128)S(1)} %copy-done.28), kind=kOutput, calls=%fused_computation.56 | convolution fusion | flops 402661376 | bytes 4194816 | tf_op jit(solution)/shard_map/ts,tkc->ksc/dot_general | solution.py:54
  186.3 4.7 %fusion.28 = f32[64,128,64]{1,2,0:T(8,128)} fusion(f32[64,64,128]{2,1,0:T(8,128)S(1)} %fusion.79, s32[64]{0:T(128)S(1)} %copy-done.29, f32[64]{0:T(128)S(1)} %compare_convert_fusion.2), kind=kOutput, calls=%fused_computation.54 | convolution fusion | flops 402661376 | bytes 4194816 | tf_op jit(solution)/shard_map/ts,tkc->ksc/dot_general | solution.py:54
  193.6 2.9 gather_fusion.10
  196.5 3.5 fusion.77
  200.0 5.1 %fusion.26 = f32[64,128,64]{1,2,0:T(8,128)} fusion(f32[64,64,128]{2,1,0:T(8,128)S(1)} %fusion.77, f32[64]{0:T(128)S(1)} %compare_convert_fusion.1, s32[64]{0:T(128)S(1)} %copy-done.30), kind=kOutput, calls=%fused_computation.52 | convolution fusion | flops 402661376 | bytes 4194816 | tf_op jit(solution)/shard_map/ts,tkc->ksc/dot_general | solution.py:54
  207.6 2.9 gather_fusion.11
  210.5 2.8 fusion.75
  213.7 5.5 %add_add_fusion.2 = f32[64,128,64]{1,2,0:T(8,128)S(1)} fusion(f32[64,128,64]{1,2,0:T(8,128)} %fusion.26, f32[64,128,64]{1,2,0:T(8,128)S(1)} %copy-done.17, f32[64,128,64]{1,2,0:T(8,128)S(1)} %copy-done.20, f32[64,64,128]{2,1,0:T(8,128)S(1)} %fusion.75, f32[64]{0:T(128)S(1)} %compare_convert_fusion, s32[64]{0:T(128)S(1)} %collective-permute-done.4), kind=kOutput, calls=%fused_computation.77 | convolution fusion | flops 404234240 | bytes 10486272 | tf_op jit(solution)/shard_map/ts,tkc->ksc/dot_general | solution.py:54
  219.2 6.0 %fusion.309 = bf16[64,8192]{1,0:T(8,128)(2,1)} fusion(f32[8,8,64,128]{3,2,1,0:T(8,128)S(1)} %bitcast.309, bf16[64,8192]{1,0:T(8,128)(2,1)S(1)} %copy-done.9, f32[8,8,64,128]{3,2,1,0:T(8,128)S(1)} %bitcast.314, f32[8,8,64,128]{3,2,1,0:T(8,128)S(1)} %bitcast.312), kind=kLoop, calls=%fused_computation.373 | loop fusion | flops 6815744 | bytes 8388608 | tf_op jit(solution)/shard_map/convert_element_type | solution.py:103
  229.1 2.9 gather_fusion.12
  232.0 2.9 gather_fusion.13
  234.9 7.1 %collective-permute-start.11 = (bf16[64,8192]{1,0:T(8,128)(2,1)}, bf16[64,8192]{1,0:T(8,128)(2,1)}, u32[]{:S(2)}, u32[]{:S(2)}) collective-permute-start(bf16[64,8192]{1,0:T(8,128)(2,1)} %fusion.309), channel_id=1, source_target_pairs={{0,1},{1,2},{2,3},{3,4},{4,5},{5,6},{6,7},{7,8},{8,9},{9,10},{10,1... | collective-permute-start | bytes 3145736 | tf_op jit(solution)/shard_map/ppermute | solution.py:27
  242.0 2.8 fusion.73
  244.7 4.7 %fusion.22 = f32[64,128,64]{1,2,0:T(8,128)} fusion(f32[64,64,128]{2,1,0:T(8,128)S(1)} %fusion.73, f32[64]{0:T(128)S(1)} %compare_convert_fusion.2, s32[64]{0:T(128)S(1)} %copy-done.28), kind=kOutput, calls=%fused_computation.48 | convolution fusion | flops 402661376 | bytes 4194816 | tf_op jit(solution)/shard_map/ts,tkc->ksc/dot_general | solution.py:54
  250.2 4.7 %fusion.20 = f32[64,128,64]{1,2,0:T(8,128)} fusion(f32[64,64,128]{2,1,0:T(8,128)S(1)} %fusion.71, s32[64]{0:T(128)S(1)} %copy-done.29, f32[64]{0:T(128)S(1)} %compare_convert_fusion.2), kind=kOutput, calls=%fused_computation.46 | convolution fusion | flops 402661376 | bytes 4194816 | tf_op jit(solution)/shard_map/ts,tkc->ksc/dot_general | solution.py:54
  257.4 2.9 gather_fusion.14
  260.3 3.5 fusion.69
  263.8 5.1 %fusion.18 = f32[64,128,64]{1,2,0:T(8,128)} fusion(f32[64,64,128]{2,1,0:T(8,128)S(1)} %fusion.69, f32[64]{0:T(128)S(1)} %compare_convert_fusion.1, s32[64]{0:T(128)S(1)} %copy-done.30), kind=kOutput, calls=%fused_computation.44 | convolution fusion | flops 402661376 | bytes 4194816 | tf_op jit(solution)/shard_map/ts,tkc->ksc/dot_general | solution.py:54
  271.4 2.9 gather_fusion.15
  274.3 2.8 fusion.67
  277.4 5.5 %add_add_fusion.1 = f32[64,128,64]{1,2,0:T(8,128)S(1)} fusion(f32[64,128,64]{1,2,0:T(8,128)} %fusion.18, f32[64,128,64]{1,2,0:T(8,128)S(1)} %copy-done.18, f32[64,128,64]{1,2,0:T(8,128)S(1)} %copy-done.21, f32[64,64,128]{2,1,0:T(8,128)S(1)} %fusion.67, f32[64]{0:T(128)S(1)} %compare_convert_fusion, s32[64]{0:T(128)S(1)} %collective-permute-done.4), kind=kOutput, calls=%fused_computation.76 | convolution fusion | flops 404234240 | bytes 10486272 | tf_op jit(solution)/shard_map/ts,tkc->ksc/dot_general | solution.py:54
  283.0 10.0 %fusion.311 = (bf16[64,8192]{1,0:T(8,128)(2,1)}, f32[64,8192]{1,0:T(8,128)}) fusion(f32[8,8,64,128]{3,2,1,0:T(8,128)S(1)} %bitcast.317, f32[8,8,64,128]{3,2,1,0:T(8,128)S(1)} %bitcast.315, f32[8,8,64,128]{3,2,1,0:T(8,128)S(1)} %bitcast.313, f32[8,8,64,128]{3,2,1,0:T(8,128)S(1)} %bitcast.310, bf16[64,8192]{1,0:T(8,128)(2,1)S(1)} %copy-done.9), kind=kLoop, calls=%fused_computation.375 | loop fusion | flops 8912896 | bytes 12582912 | tf_op jit(solution)/shard_map/convert_element_type | solution.py:110
  299.1 6.7 %collective-permute-start.13 = (bf16[64,8192]{1,0:T(8,128)(2,1)}, bf16[64,8192]{1,0:T(8,128)(2,1)}, u32[]{:S(2)}, u32[]{:S(2)}) collective-permute-start(bf16[64,8192]{1,0:T(8,128)(2,1)} %get-tuple-element.12), channel_id=1, source_target_pairs={{0,1},{1,2},{2,3},{3,4},{4,5},{5,6},{6,7},{7,8},{8,9},{9,10},{10,1... | collective-permute-start | bytes 3145736 | tf_op jit(solution)/shard_map/ppermute | solution.py:27
  308.5 4.7 %fusion.14 = f32[64,128,64]{1,2,0:T(8,128)} fusion(f32[64,64,128]{2,1,0:T(8,128)S(1)} %fusion.65, f32[64]{0:T(128)S(1)} %compare_convert_fusion.2, s32[64]{0:T(128)S(1)} %copy-done.28), kind=kOutput, calls=%fused_computation.40 | convolution fusion | flops 402661376 | bytes 4194816 | tf_op jit(solution)/shard_map/ts,tkc->ksc/dot_general | solution.py:54
  315.8 4.7 %fusion.12 = f32[64,128,64]{1,2,0:T(8,128)} fusion(f32[64,64,128]{2,1,0:T(8,128)S(1)} %fusion.63, s32[64]{0:T(128)S(1)} %copy-done.29, f32[64]{0:T(128)S(1)} %compare_convert_fusion.2), kind=kOutput, calls=%fused_computation.38 | convolution fusion | flops 402661376 | bytes 4194816 | tf_op jit(solution)/shard_map/ts,tkc->ksc/dot_general | solution.py:54
  323.7 3.5 fusion.61
  327.1 4.8 %fusion.10 = f32[64,128,64]{1,2,0:T(8,128)} fusion(f32[64,64,128]{2,1,0:T(8,128)S(1)} %fusion.61, f32[64]{0:T(128)S(1)} %compare_convert_fusion.1, s32[64]{0:T(128)S(1)} %copy-done.30), kind=kOutput, calls=%fused_computation.36 | convolution fusion | flops 402661376 | bytes 4194816 | tf_op jit(solution)/shard_map/ts,tkc->ksc/dot_general | solution.py:54
  335.2 2.8 fusion.59
  338.4 5.4 %add_add_fusion = f32[64,128,64]{1,2,0:T(8,128)S(1)} fusion(f32[64,128,64]{1,2,0:T(8,128)} %fusion.10, f32[64,128,64]{1,2,0:T(8,128)S(1)} %copy-done.14, f32[64,128,64]{1,2,0:T(8,128)S(1)} %copy-done.15, f32[64,64,128]{2,1,0:T(8,128)S(1)} %fusion.59, f32[64]{0:T(128)S(1)} %compare_convert_fusion, s32[64]{0:T(128)S(1)} %collective-permute-done.4), kind=kOutput, calls=%fused_computation.74 | convolution fusion | flops 404234240 | bytes 10486272 | tf_op jit(solution)/shard_map/ts,tkc->ksc/dot_general | solution.py:54
  343.7 4.1 fusion.1
  347.8 30.2 %all-reduce.2 = (f32[64,64]{0,1:T(8,128)S(1)}, f32[64,64]{0,1:T(8,128)S(1)}) all-reduce(f32[64,64]{0,1:T(8,128)S(1)} %fusion.313, f32[64,64]{0,1:T(8,128)S(1)} %fusion.1), channel_id=1, replica_groups=mesh['grp_0'=4,'grp_1'=2,'row_0'=4,'row_1'=4] {'grp_0'}, use_global_device_ids=true, to_apply=%region_0.2 | all-reduce | flops 8192 | bytes 65536 | tf_op jit(solution)/shard_map/psum | solution.py:41
  378.0 3.6 all-reduce.3
  381.6 14.9 %all-reduce.1 = (f32[64,64]{0,1:T(8,128)S(1)}, f32[64,64]{0,1:T(8,128)S(1)}) all-reduce(f32[64,64]{0,1:T(8,128)S(1)} %get-tuple-element.10, f32[64,64]{0,1:T(8,128)S(1)} %get-tuple-element.11), channel_id=1, replica_groups=mesh['grp_0'=4,'grp_1'=2,'row_0'=4,'row_1'=4] {'row_0'}, use_global_device_ids=true, to_apply=%region_2.4 | all-reduce | flops 8192 | bytes 65536 | tf_op jit(solution)/shard_map/psum | solution.py:41
  396.5 23.3 %all-reduce = (f32[64,64]{0,1:T(8,128)S(1)}, f32[64,64]{0,1:T(8,128)S(1)}) all-reduce(f32[64,64]{0,1:T(8,128)S(1)} %get-tuple-element.6, f32[64,64]{0,1:T(8,128)S(1)} %get-tuple-element.7), channel_id=1, replica_groups=mesh['grp_0'=4,'grp_1'=2,'row_0'=4,'row_1'=4] {'row_1'}, use_global_device_ids=true, to_apply=%region_3.5 | all-reduce | flops 8192 | bytes 65536 | tf_op jit(solution)/shard_map/psum | solution.py:41
  419.9 5.8 %cholesky.15 = f32[64,64]{1,0:T(8,128)S(1)} custom-call(f32[64,64]{1,0:T(8,128)S(1)} %fusion.165), custom_call_target="Cholesky" | custom-call | tf_op jit(solution)/shard_map/jit(cholesky)/cholesky | solution.py:121
  427.1 4.9 %custom-call.10 = f32[1,64,64]{1,2,0:T(8,128)S(1)} custom-call(f32[1,64,64]{2,1,0:T(8,128)S(1)} %fusion.159), custom_call_target="InvertDiagBlocksLowerTriangular" | custom-call | tf_op jit(solution)/shard_map/jit(_solve_triangular)/triangular_solve | solution.py:122
  432.0 4.8 %fusion.163 = f32[64,8192]{1,0:T(8,128)} fusion(f32[64,8192]{1,0:T(8,128)} %get-tuple-element.13, f32[1,64,64]{1,2,0:T(8,128)S(1)} %custom-call.10), kind=kOutput, calls=%fused_computation.202 | convolution fusion | flops 402653184 | bytes 4210688 | tf_op jit(solution)/shard_map/jit(_solve_triangular)/triangular_solve | solution.py:122
  (139 shorter events, 76.7 us)
Async XLA Ops:
  0.6 25.4 %copy-start = (bf16[64,128,128]{2,1,0:T(8,128)(2,1)S(1)}, bf16[64,128,128]{2,1,0:T(8,128)(2,1)}, u32[]{:S(2)}) copy-start(bf16[64,128,128]{2,1,0:T(8,128)(2,1)} %param.14) | copy-start | bytes 6291460
  0.6 21.3 %copy-start.29 = (s32[64]{0:T(128)S(1)}, s32[64]{0:T(128)}, u32[]{:S(2)}) copy-start(s32[64]{0:T(128)} %param.16) | copy-start | bytes 772
  0.7 21.3 %copy-start.28 = (s32[64]{0:T(128)S(1)}, s32[64]{0:T(128)}, u32[]{:S(2)}) copy-start(s32[64]{0:T(128)} %param.15) | copy-start | bytes 772
  0.7 78.3 %collective-permute-start = (bf16[64,8192]{1,0:T(8,128)(2,1)}, bf16[64,8192]{1,0:T(8,128)(2,1)}, u32[]{:S(2)}, u32[]{:S(2)}) collective-permute-start(bf16[64,8192]{1,0:T(8,128)(2,1)} %param.13), channel_id=1, source_target_pairs={{1,0},{2,1},{3,2},{4,3},{5,4},{6,5},{7,6},{8,7},{9,8},{10,9},{11,1... | collective-permute-start | bytes 3145736 | tf_op jit(solution)/shard_map/ppermute | solution.py:28
  2.1 80.1 %collective-permute-start.1 = (bf16[64,8192]{1,0:T(8,128)(2,1)}, bf16[64,8192]{1,0:T(8,128)(2,1)}, u32[]{:S(2)}, u32[]{:S(2)}) collective-permute-start(bf16[64,8192]{1,0:T(8,128)(2,1)} %param.13), channel_id=1, source_target_pairs={{0,1},{1,2},{2,3},{3,4},{4,5},{5,6},{6,7},{7,8},{8,9},{9,10},{10,1... | collective-permute-start | bytes 3145736 | tf_op jit(solution)/shard_map/ppermute | solution.py:27
  7.7 84.5 %collective-permute-start.3 = (bf16[64,128,128]{2,1,0:T(8,128)(2,1)}, bf16[64,128,128]{2,1,0:T(8,128)(2,1)}, u32[]{:S(2)}, u32[]{:S(2)}) collective-permute-start(bf16[64,128,128]{2,1,0:T(8,128)(2,1)} %param.18), channel_id=1, source_target_pairs={{0,1},{1,2},{2,3},{3,4},{4,5},{5,6},{6,7},{7,8},{8,9},{9,10},{10,1... | collective-permute-start | bytes 6291464 | tf_op jit(solution)/shard_map/ppermute | solution.py:16
  11.6 59.8 %collective-permute-start.5 = (s32[1]{0:T(128)}, s32[1]{0:T(128)}, u32[]{:S(2)}, u32[]{:S(2)}) collective-permute-start(s32[1]{0:T(128)} %param.21), channel_id=1, source_target_pairs={{0,1},{1,2},{2,3},{3,4},{4,5},{5,6},{6,7},{7,8},{8,9},{9,10},{10,1... | collective-permute-start | bytes 20 | tf_op jit(solution)/shard_map/ppermute | solution.py:16
  14.3 80.4 %collective-permute-start.4 = (s32[64]{0:T(128)}, s32[64]{0:T(128)S(1)}, u32[]{:S(2)}, u32[]{:S(2)}) collective-permute-start(s32[64]{0:T(128)} %param.20), channel_id=1, source_target_pairs={{0,1},{1,2},{2,3},{3,4},{4,5},{5,6},{6,7},{7,8},{8,9},{9,10},{10,1... | collective-permute-start | bytes 776 | tf_op jit(solution)/shard_map/ppermute | solution.py:16
  28.8 4.7 %copy-start.27 = (bf16[64,64,128]{2,1,0:T(8,128)(2,1)S(1)}, bf16[64,64,128]{2,1,0:T(8,128)(2,1)}, u32[]{:S(2)}) copy-start(bf16[64,64,128]{2,1,0:T(8,128)(2,1)} %gather_fusion.1) | copy-start | bytes 3145732
  34.1 4.7 %copy-start.31 = (s32[64]{0:T(128)S(1)}, s32[64]{0:T(128)}, u32[]{:S(2)}) copy-start(s32[64]{0:T(128)} %param.20) | copy-start | bytes 772
  34.2 37.3 %copy-start.30 = (s32[64]{0:T(128)S(1)}, s32[64]{0:T(128)}, u32[]{:S(2)}) copy-start(s32[64]{0:T(128)} %param.19) | copy-start | bytes 772
  71.4 7.5 %collective-permute-start.2 = (s32[64]{0:T(128)S(1)}, s32[64]{0:T(128)S(1)}, u32[]{:S(2)}, u32[]{:S(2)}) collective-permute-start(s32[64]{0:T(128)S(1)} %copy-done.30), channel_id=1, source_target_pairs={{0,1},{1,2},{2,3},{3,4},{4,5},{5,6},{6,7},{7,8},{8,9},{9,10},{10,1... | collective-permute-start | bytes 776 | tf_op jit(solution)/shard_map/ppermute | solution.py:16
  88.8 3.4 copy-start.26
  92.2 2.5 copy-start.12
  92.2 2.8 copy-start.13
  94.7 4.1 copy-start.9
  98.8 2.5 copy-start.1
  101.3 28.9 %collective-permute-start.6 = (bf16[64,8192]{1,0:T(8,128)(2,1)}, bf16[64,8192]{1,0:T(8,128)(2,1)}, u32[]{:S(2)}, u32[]{:S(2)}) collective-permute-start(bf16[64,8192]{1,0:T(8,128)(2,1)} %multiply_convert_fusion), channel_id=1, source_target_pairs={{1,0},{2,1},{3,2},{4,3},{5,4},{6,5},{7,6},{8,7},{9,8},{10,9},{11,1... | collective-permute-start | bytes 3145736 | tf_op jit(solution)/shard_map/ppermute | solution.py:28
  111.0 33.1 %collective-permute-start.7 = (bf16[64,8192]{1,0:T(8,128)(2,1)}, bf16[64,8192]{1,0:T(8,128)(2,1)}, u32[]{:S(2)}, u32[]{:S(2)}) collective-permute-start(bf16[64,8192]{1,0:T(8,128)(2,1)} %multiply_convert_fusion), channel_id=1, source_target_pairs={{0,1},{1,2},{2,3},{3,4},{4,5},{5,6},{6,7},{7,8},{8,9},{9,10},{10,1... | collective-permute-start | bytes 3145736 | tf_op jit(solution)/shard_map/ppermute | solution.py:27
  120.2 4.7 %copy-start.23 = (bf16[64,64,128]{2,1,0:T(8,128)(2,1)S(1)}, bf16[64,64,128]{2,1,0:T(8,128)(2,1)}, u32[]{:S(2)}) copy-start(bf16[64,64,128]{2,1,0:T(8,128)(2,1)} %gather_fusion.5) | copy-start | bytes 3145732
  149.6 2.8 copy-start.16
  149.6 3.2 copy-start.19
  152.7 5.6 %copy-start.2 = (f32[64,128,64]{1,2,0:T(8,128)S(1)}, f32[64,128,64]{1,2,0:T(8,128)}, u32[]{:S(2)}) copy-start(f32[64,128,64]{1,2,0:T(8,128)} %copy-done.1) | copy-start | bytes 6291460
  158.3 4.4 %copy-start.6 = (f32[64,128,64]{1,2,0:T(8,128)}, f32[64,128,64]{1,2,0:T(8,128)S(1)}, u32[]{:S(2)}) copy-start(f32[64,128,64]{1,2,0:T(8,128)S(1)} %add_add_fusion.3) | copy-start | bytes 6291460
  162.7 28.4 %collective-permute-start.8 = (bf16[64,8192]{1,0:T(8,128)(2,1)}, bf16[64,8192]{1,0:T(8,128)(2,1)}, u32[]{:S(2)}, u32[]{:S(2)}) collective-permute-start(bf16[64,8192]{1,0:T(8,128)(2,1)} %fusion.310), channel_id=1, source_target_pairs={{1,0},{2,1},{3,2},{4,3},{5,4},{6,5},{7,6},{8,7},{9,8},{10,9},{11,1... | collective-permute-start | bytes 3145736 | tf_op jit(solution)/shard_map/ppermute | solution.py:28
  172.4 32.7 %collective-permute-start.9 = (bf16[64,8192]{1,0:T(8,128)(2,1)}, bf16[64,8192]{1,0:T(8,128)(2,1)}, u32[]{:S(2)}, u32[]{:S(2)}) collective-permute-start(bf16[64,8192]{1,0:T(8,128)(2,1)} %fusion.310), channel_id=1, source_target_pairs={{0,1},{1,2},{2,3},{3,4},{4,5},{5,6},{6,7},{7,8},{8,9},{9,10},{10,1... | collective-permute-start | bytes 3145736 | tf_op jit(solution)/shard_map/ppermute | solution.py:27
  180.9 4.7 %copy-start.24 = (bf16[64,64,128]{2,1,0:T(8,128)(2,1)S(1)}, bf16[64,64,128]{2,1,0:T(8,128)(2,1)}, u32[]{:S(2)}) copy-start(bf16[64,64,128]{2,1,0:T(8,128)(2,1)} %gather_fusion.9) | copy-start | bytes 3145732
  210.5 2.8 copy-start.17
  210.5 3.2 copy-start.20
  213.7 5.5 %copy-start.3 = (f32[64,128,64]{1,2,0:T(8,128)S(1)}, f32[64,128,64]{1,2,0:T(8,128)}, u32[]{:S(2)}) copy-start(f32[64,128,64]{1,2,0:T(8,128)} %copy-done.1) | copy-start | bytes 6291460
  213.7 5.5 %copy-start.7 = (f32[64,128,64]{1,2,0:T(8,128)S(1)}, f32[64,128,64]{1,2,0:T(8,128)}, u32[]{:S(2)}) copy-start(f32[64,128,64]{1,2,0:T(8,128)} %copy-done.6) | copy-start | bytes 6291460
  219.2 6.0 %copy-start.10 = (f32[64,128,64]{1,2,0:T(8,128)}, f32[64,128,64]{1,2,0:T(8,128)S(1)}, u32[]{:S(2)}) copy-start(f32[64,128,64]{1,2,0:T(8,128)S(1)} %add_add_fusion.2) | copy-start | bytes 6291460
  225.2 29.6 %collective-permute-start.10 = (bf16[64,8192]{1,0:T(8,128)(2,1)}, bf16[64,8192]{1,0:T(8,128)(2,1)}, u32[]{:S(2)}, u32[]{:S(2)}) collective-permute-start(bf16[64,8192]{1,0:T(8,128)(2,1)} %fusion.309), channel_id=1, source_target_pairs={{1,0},{2,1},{3,2},{4,3},{5,4},{6,5},{7,6},{8,7},{9,8},{10,9},{11,1... | collective-permute-start | bytes 3145736 | tf_op jit(solution)/shard_map/ppermute | solution.py:28
  234.9 34.0 %collective-permute-start.11 = (bf16[64,8192]{1,0:T(8,128)(2,1)}, bf16[64,8192]{1,0:T(8,128)(2,1)}, u32[]{:S(2)}, u32[]{:S(2)}) collective-permute-start(bf16[64,8192]{1,0:T(8,128)(2,1)} %fusion.309), channel_id=1, source_target_pairs={{0,1},{1,2},{2,3},{3,4},{4,5},{5,6},{6,7},{7,8},{8,9},{9,10},{10,1... | collective-permute-start | bytes 3145736 | tf_op jit(solution)/shard_map/ppermute | solution.py:27
  244.7 4.7 %copy-start.25 = (bf16[64,64,128]{2,1,0:T(8,128)(2,1)S(1)}, bf16[64,64,128]{2,1,0:T(8,128)(2,1)}, u32[]{:S(2)}) copy-start(bf16[64,64,128]{2,1,0:T(8,128)(2,1)} %gather_fusion.13) | copy-start | bytes 3145732
  274.3 2.8 copy-start.18
  274.3 3.2 copy-start.21
  277.4 5.5 %copy-start.4 = (f32[64,128,64]{1,2,0:T(8,128)S(1)}, f32[64,128,64]{1,2,0:T(8,128)}, u32[]{:S(2)}) copy-start(f32[64,128,64]{1,2,0:T(8,128)} %copy-done.1) | copy-start | bytes 6291460
  277.4 5.5 %copy-start.8 = (f32[64,128,64]{1,2,0:T(8,128)S(1)}, f32[64,128,64]{1,2,0:T(8,128)}, u32[]{:S(2)}) copy-start(f32[64,128,64]{1,2,0:T(8,128)} %copy-done.6) | copy-start | bytes 6291460
  277.4 5.5 %copy-start.11 = (f32[64,128,64]{1,2,0:T(8,128)S(1)}, f32[64,128,64]{1,2,0:T(8,128)}, u32[]{:S(2)}) copy-start(f32[64,128,64]{1,2,0:T(8,128)} %copy-done.10) | copy-start | bytes 6291460
  293.0 27.5 %collective-permute-start.12 = (bf16[64,8192]{1,0:T(8,128)(2,1)}, bf16[64,8192]{1,0:T(8,128)(2,1)}, u32[]{:S(2)}, u32[]{:S(2)}) collective-permute-start(bf16[64,8192]{1,0:T(8,128)(2,1)} %get-tuple-element.12), channel_id=1, source_target_pairs={{1,0},{2,1},{3,2},{4,3},{5,4},{6,5},{7,6},{8,7},{9,8},{10,9},{11,1... | collective-permute-start | bytes 3145736 | tf_op jit(solution)/shard_map/ppermute | solution.py:28
  299.1 32.9 %collective-permute-start.13 = (bf16[64,8192]{1,0:T(8,128)(2,1)}, bf16[64,8192]{1,0:T(8,128)(2,1)}, u32[]{:S(2)}, u32[]{:S(2)}) collective-permute-start(bf16[64,8192]{1,0:T(8,128)(2,1)} %get-tuple-element.12), channel_id=1, source_target_pairs={{0,1},{1,2},{2,3},{3,4},{4,5},{5,6},{6,7},{7,8},{8,9},{9,10},{10,1... | collective-permute-start | bytes 3145736 | tf_op jit(solution)/shard_map/ppermute | solution.py:27
  308.5 4.7 %copy-start.5 = (f32[64,8192]{1,0:T(8,128)S(1)}, f32[64,8192]{1,0:T(8,128)}, u32[]{:S(2)}) copy-start(f32[64,8192]{1,0:T(8,128)} %get-tuple-element.13) | copy-start | bytes 6291460
  313.2 1.8 copy-start.22
  335.2 2.8 copy-start.14
  335.2 3.2 copy-start.15
where the time goes:
time: 447 us; the launch traced here: 438 us
  matrix products  156 us (35%)
  local copies, waits for them, and re-layouts  82.1 us (18%)
  blocking collectives  72 us (16%)
  starting transfers between devices  55.8 us (12%)
  other arithmetic  36.3 us (8%)
  waiting for transfers between devices  33.1 us (7%)
    dot_general x20, matrix products, place(): jnp.einsum('ts,tkc->ksc', selector, terms, precision=lax.Precision.HIGHES...  95.9 us
    psum x4, blocking collectives, over_axes(): array = lax.psum(array, axis)  72 us
    gather x20, local copies, waits for them, and re-layouts, tile_terms(): picked = jnp.take(blocks, index, axis=1)  48.2 us
    ppermute x4, waiting for transfers between devices, from_behind(): return lax.ppermute(array, axis, pairs)  33 us
    ppermute x5, starting transfers between devices, extended(): lax.ppermute(last, axis, up)  31.5 us
    dot_general x10, matrix products, tile_terms(): jnp.einsum('ktc,trc->tkr', picked, tiles, preferred_element_type=jnp.floa...  31.1 us
    ppermute x4, starting transfers between devices, from_behind(): return lax.ppermute(array, axis, pairs)  17.8 us
    dot_general x10, matrix products, tile_terms(): jnp.einsum('ktr,trc->tkc', picked, tiles, preferred_element_type=jnp.floa...  17.3 us
  transfers between devices with their start and end apart: 14, of which 2 were waited for; matrix products, arithmetic and copies ran while one was open for 39% of the time, Pallas kernels for 0%

commit v1 on v0

--- a/solution.py
+++ b/solution.py
@@ -38,7 +38,7 @@
 
 def over_axes(array, axes):
     for axis in axes:
-        array = lax.psum(array, axis)
+        array = jnp.sum(lax.all_gather(array, axis), axis=0)
     return array
 
 

time: 447 us -> 471 us (1.054)
  blocking collectives: 72 us -> 95.2 us
    all_gather x0 -> x8, blocking collectives: none -> 95.2 us  [over_axes(): array = jnp.sum(lax.all_gather(array, axis), axis=0)]
    psum x4 -> x0, blocking collectives: 72 us -> none  [over_axes(): array = lax.psum(array, axis)]
  transfers between devices with their start and end apart: 14 -> 14, of which waited for: 2 -> 2; matrix products, arithmetic and copies ran while one was open for 39% -> 41% of each run, Pallas kernels for 0% -> 0%
where the time goes in v1:
time: 471 us; the launch traced here: 463 us
  matrix products  157 us (33%)
  blocking collectives  95.2 us (20%)
  local copies, waits for them, and re-layouts  82.2 us (17%)
  starting transfers between devices  55.9 us (12%)
  other arithmetic  36.5 us (8%)
  waiting for transfers between devices  33.1 us (7%)
    dot_general x20, matrix products, place(): jnp.einsum('ts,tkc->ksc', selector, terms, precision=lax.Precision.HIGHES...  95.4 us
    all_gather x8, blocking collectives, over_axes(): array = jnp.sum(lax.all_gather(array, axis), axis=0)  95.2 us
    gather x20, local copies, waits for them, and re-layouts, tile_terms(): picked = jnp.take(blocks, index, axis=1)  48.3 us
    ppermute x4, waiting for transfers between devices, from_behind(): return lax.ppermute(array, axis, pairs)  33.1 us
    ppermute x5, starting transfers between devices, extended(): lax.ppermute(last, axis, up)  31.5 us
    dot_general x10, matrix products, tile_terms(): jnp.einsum('ktc,trc->tkr', picked, tiles, preferred_element_type=jnp.floa...  29.9 us
    ppermute x4, starting transfers between devices, from_behind(): return lax.ppermute(array, axis, pairs)  17.8 us
    dot_general x10, matrix products, tile_terms(): jnp.einsum('ktr,trc->tkc', picked, tiles, preferred_element_type=jnp.floa...  17.3 us
  transfers between devices with their start and end apart: 14, of which 2 were waited for; matrix products, arithmetic and copies ran while one was open for 41% of the time, Pallas kernels for 0%

profile of v1, /device:TPU:0, one launch (start us, length us, event | category | flops | bytes accessed | tf_op | source)
XLA Modules:
  0.0 462.8 jit_solution(11637986331984955919)
XLA Ops:
  2.1 5.5 %collective-permute-start.1 = (bf16[64,8192]{1,0:T(8,128)(2,1)}, bf16[64,8192]{1,0:T(8,128)(2,1)}, u32[]{:S(2)}, u32[]{:S(2)}) collective-permute-start(bf16[64,8192]{1,0:T(8,128)(2,1)} %param.13), channel_id=1, source_target_pairs={{0,1},{1,2},{2,3},{3,4},{4,5},{5,6},{6,7},{7,8},{8,9},{9,10},{10,1... | collective-permute-start | bytes 3145736 | tf_op jit(solution)/shard_map/ppermute | solution.py:27
  7.6 4.0 collective-permute-start.3
  14.3 4.8 %collective-permute-start.4 = (s32[64]{0:T(128)}, s32[64]{0:T(128)S(1)}, u32[]{:S(2)}, u32[]{:S(2)}) collective-permute-start(s32[64]{0:T(128)} %param.20), channel_id=1, source_target_pairs={{0,1},{1,2},{2,3},{3,4},{4,5},{5,6},{6,7},{7,8},{8,9},{9,10},{10,1... | collective-permute-start | bytes 776 | tf_op jit(solution)/shard_map/ppermute | solution.py:16
  28.7 4.6 %fusion.46 = f32[64,128,64]{1,2,0:T(8,128)} fusion(f32[64,64,128]{2,1,0:T(8,128)S(1)} %fusion.97, f32[64]{0:T(128)S(1)} %compare_convert_fusion.2, s32[64]{0:T(128)S(1)} %copy-done.28), kind=kOutput, calls=%fused_computation.72 | convolution fusion | flops 402661376 | bytes 4194816 | tf_op jit(solution)/shard_map/ts,tkc->ksc/dot_general | solution.py:54
  34.1 4.6 %fusion.44 = f32[64,128,64]{1,2,0:T(8,128)} fusion(f32[64,64,128]{2,1,0:T(8,128)S(1)} %fusion.95, s32[64]{0:T(128)S(1)} %copy-done.29, f32[64]{0:T(128)S(1)} %compare_convert_fusion.2), kind=kOutput, calls=%fused_computation.70 | convolution fusion | flops 402661376 | bytes 4194816 | tf_op jit(solution)/shard_map/ts,tkc->ksc/dot_general | solution.py:54
  38.8 32.6 %collective-permute-done.5 = s32[1]{0:T(128)} collective-permute-done((s32[1]{0:T(128)}, s32[1]{0:T(128)}, u32[]{:S(2)}, u32[]{:S(2)}) %collective-permute-start.5) | collective-permute-done | bytes 36 | tf_op jit(solution)/shard_map/ppermute | solution.py:16
  71.4 6.4 %collective-permute-start.2 = (s32[64]{0:T(128)S(1)}, s32[64]{0:T(128)S(1)}, u32[]{:S(2)}, u32[]{:S(2)}) collective-permute-start(s32[64]{0:T(128)S(1)} %copy-done.30), channel_id=1, source_target_pairs={{0,1},{1,2},{2,3},{3,4},{4,5},{5,6},{6,7},{7,8},{8,9},{9,10},{10,1... | collective-permute-start | bytes 776 | tf_op jit(solution)/shard_map/ppermute | solution.py:16
  85.3 3.5 fusion.93
  88.8 3.3 fusion.42
  95.0 3.8 add_add_fusion.4
  105.1 2.9 gather_fusion.4
  108.0 2.9 gather_fusion.5
  110.9 6.5 %collective-permute-start.7 = (bf16[64,8192]{1,0:T(8,128)(2,1)}, bf16[64,8192]{1,0:T(8,128)(2,1)}, u32[]{:S(2)}, u32[]{:S(2)}) collective-permute-start(bf16[64,8192]{1,0:T(8,128)(2,1)} %multiply_convert_fusion), channel_id=1, source_target_pairs={{0,1},{1,2},{2,3},{3,4},{4,5},{5,6},{6,7},{7,8},{8,9},{9,10},{10,1... | collective-permute-start | bytes 3145736 | tf_op jit(solution)/shard_map/ppermute | solution.py:27
  120.2 4.6 %fusion.38 = f32[64,128,64]{1,2,0:T(8,128)} fusion(f32[64,64,128]{2,1,0:T(8,128)S(1)} %fusion.89, f32[64]{0:T(128)S(1)} %compare_convert_fusion.2, s32[64]{0:T(128)S(1)} %copy-done.28), kind=kOutput, calls=%fused_computation.64 | convolution fusion | flops 402661376 | bytes 4194816 | tf_op jit(solution)/shard_map/ts,tkc->ksc/dot_general | solution.py:54
  125.6 4.7 %fusion.36 = f32[64,128,64]{1,2,0:T(8,128)} fusion(f32[64,64,128]{2,1,0:T(8,128)S(1)} %fusion.87, s32[64]{0:T(128)S(1)} %copy-done.29, f32[64]{0:T(128)S(1)} %compare_convert_fusion.2), kind=kOutput, calls=%fused_computation.62 | convolution fusion | flops 402661376 | bytes 4194816 | tf_op jit(solution)/shard_map/ts,tkc->ksc/dot_general | solution.py:54
  132.8 2.9 gather_fusion.6
  135.7 3.5 fusion.85
  139.2 4.9 %fusion.34 = f32[64,128,64]{1,2,0:T(8,128)} fusion(f32[64,64,128]{2,1,0:T(8,128)S(1)} %fusion.85, f32[64]{0:T(128)S(1)} %compare_convert_fusion.1, s32[64]{0:T(128)S(1)} %copy-done.30), kind=kOutput, calls=%fused_computation.60 | convolution fusion | flops 402661376 | bytes 4194816 | tf_op jit(solution)/shard_map/ts,tkc->ksc/dot_general | solution.py:54
  146.6 2.9 gather_fusion.7
  149.5 2.8 fusion.83
  152.7 5.5 %add_add_fusion.3 = f32[64,128,64]{1,2,0:T(8,128)S(1)} fusion(f32[64,128,64]{1,2,0:T(8,128)} %fusion.34, f32[64,128,64]{1,2,0:T(8,128)S(1)} %copy-done.15, f32[64,128,64]{1,2,0:T(8,128)S(1)} %copy-done.18, f32[64,64,128]{2,1,0:T(8,128)S(1)} %fusion.83, f32[64]{0:T(128)S(1)} %compare_convert_fusion, s32[64]{0:T(128)S(1)} %collective-permute-done.4), kind=kOutput, calls=%fused_computation.78 | convolution fusion | flops 404234240 | bytes 10486272 | tf_op jit(solution)/shard_map/ts,tkc->ksc/dot_general | solution.py:54
  158.2 4.4 fusion.310
  166.5 2.9 gather_fusion.8
  169.3 2.9 gather_fusion.9
  172.2 5.7 %collective-permute-start.9 = (bf16[64,8192]{1,0:T(8,128)(2,1)}, bf16[64,8192]{1,0:T(8,128)(2,1)}, u32[]{:S(2)}, u32[]{:S(2)}) collective-permute-start(bf16[64,8192]{1,0:T(8,128)(2,1)} %fusion.310), channel_id=1, source_target_pairs={{0,1},{1,2},{2,3},{3,4},{4,5},{5,6},{6,7},{7,8},{8,9},{9,10},{10,1... | collective-permute-start | bytes 3145736 | tf_op jit(solution)/shard_map/ppermute | solution.py:27
  180.7 4.7 %fusion.30 = f32[64,128,64]{1,2,0:T(8,128)} fusion(f32[64,64,128]{2,1,0:T(8,128)S(1)} %fusion.81, f32[64]{0:T(128)S(1)} %compare_convert_fusion.2, s32[64]{0:T(128)S(1)} %copy-done.28), kind=kOutput, calls=%fused_computation.56 | convolution fusion | flops 402661376 | bytes 4194816 | tf_op jit(solution)/shard_map/ts,tkc->ksc/dot_general | solution.py:54
  186.2 4.7 %fusion.28 = f32[64,128,64]{1,2,0:T(8,128)} fusion(f32[64,64,128]{2,1,0:T(8,128)S(1)} %fusion.79, s32[64]{0:T(128)S(1)} %copy-done.29, f32[64]{0:T(128)S(1)} %compare_convert_fusion.2), kind=kOutput, calls=%fused_computation.54 | convolution fusion | flops 402661376 | bytes 4194816 | tf_op jit(solution)/shard_map/ts,tkc->ksc/dot_general | solution.py:54
  193.3 3.0 gather_fusion.10
  196.3 3.5 fusion.77
  199.7 5.1 %fusion.26 = f32[64,128,64]{1,2,0:T(8,128)} fusion(f32[64,64,128]{2,1,0:T(8,128)S(1)} %fusion.77, f32[64]{0:T(128)S(1)} %compare_convert_fusion.1, s32[64]{0:T(128)S(1)} %copy-done.30), kind=kOutput, calls=%fused_computation.52 | convolution fusion | flops 402661376 | bytes 4194816 | tf_op jit(solution)/shard_map/ts,tkc->ksc/dot_general | solution.py:54
  207.4 2.9 gather_fusion.11
  210.3 2.8 fusion.75
  213.4 5.5 %add_add_fusion.2 = f32[64,128,64]{1,2,0:T(8,128)S(1)} fusion(f32[64,128,64]{1,2,0:T(8,128)} %fusion.26, f32[64,128,64]{1,2,0:T(8,128)S(1)} %copy-done.16, f32[64,128,64]{1,2,0:T(8,128)S(1)} %copy-done.19, f32[64,64,128]{2,1,0:T(8,128)S(1)} %fusion.75, f32[64]{0:T(128)S(1)} %compare_convert_fusion, s32[64]{0:T(128)S(1)} %collective-permute-done.4), kind=kOutput, calls=%fused_computation.77 | convolution fusion | flops 404234240 | bytes 10486272 | tf_op jit(solution)/shard_map/ts,tkc->ksc/dot_general | solution.py:54
  219.0 6.1 %fusion.309 = bf16[64,8192]{1,0:T(8,128)(2,1)} fusion(f32[8,8,64,128]{3,2,1,0:T(8,128)S(1)} %bitcast.317, bf16[64,8192]{1,0:T(8,128)(2,1)S(1)} %copy-done.8, f32[8,8,64,128]{3,2,1,0:T(8,128)S(1)} %bitcast.322, f32[8,8,64,128]{3,2,1,0:T(8,128)S(1)} %bitcast.320), kind=kLoop, calls=%fused_computation.372 | loop fusion | flops 6815744 | bytes 8388608 | tf_op jit(solution)/shard_map/convert_element_type | solution.py:103
  228.9 2.9 gather_fusion.12
  231.8 2.9 gather_fusion.13
  234.7 7.2 %collective-permute-start.11 = (bf16[64,8192]{1,0:T(8,128)(2,1)}, bf16[64,8192]{1,0:T(8,128)(2,1)}, u32[]{:S(2)}, u32[]{:S(2)}) collective-permute-start(bf16[64,8192]{1,0:T(8,128)(2,1)} %fusion.309), channel_id=1, source_target_pairs={{0,1},{1,2},{2,3},{3,4},{4,5},{5,6},{6,7},{7,8},{8,9},{9,10},{10,1... | collective-permute-start | bytes 3145736 | tf_op jit(solution)/shard_map/ppermute | solution.py:27
  244.7 4.7 %fusion.22 = f32[64,128,64]{1,2,0:T(8,128)} fusion(f32[64,64,128]{2,1,0:T(8,128)S(1)} %fusion.73, f32[64]{0:T(128)S(1)} %compare_convert_fusion.2, s32[64]{0:T(128)S(1)} %copy-done.28), kind=kOutput, calls=%fused_computation.48 | convolution fusion | flops 402661376 | bytes 4194816 | tf_op jit(solution)/shard_map/ts,tkc->ksc/dot_general | solution.py:54
  250.1 4.7 %fusion.20 = f32[64,128,64]{1,2,0:T(8,128)} fusion(f32[64,64,128]{2,1,0:T(8,128)S(1)} %fusion.71, s32[64]{0:T(128)S(1)} %copy-done.29, f32[64]{0:T(128)S(1)} %compare_convert_fusion.2), kind=kOutput, calls=%fused_computation.46 | convolution fusion | flops 402661376 | bytes 4194816 | tf_op jit(solution)/shard_map/ts,tkc->ksc/dot_general | solution.py:54
  257.4 2.9 gather_fusion.14
  260.2 3.5 fusion.69
  263.7 5.1 %fusion.18 = f32[64,128,64]{1,2,0:T(8,128)} fusion(f32[64,64,128]{2,1,0:T(8,128)S(1)} %fusion.69, f32[64]{0:T(128)S(1)} %compare_convert_fusion.1, s32[64]{0:T(128)S(1)} %copy-done.30), kind=kOutput, calls=%fused_computation.44 | convolution fusion | flops 402661376 | bytes 4194816 | tf_op jit(solution)/shard_map/ts,tkc->ksc/dot_general | solution.py:54
  271.3 2.9 gather_fusion.15
  274.2 2.8 fusion.67
  277.4 5.5 %add_add_fusion.1 = f32[64,128,64]{1,2,0:T(8,128)S(1)} fusion(f32[64,128,64]{1,2,0:T(8,128)} %fusion.18, f32[64,128,64]{1,2,0:T(8,128)S(1)} %copy-done.17, f32[64,128,64]{1,2,0:T(8,128)S(1)} %copy-done.20, f32[64,64,128]{2,1,0:T(8,128)S(1)} %fusion.67, f32[64]{0:T(128)S(1)} %compare_convert_fusion, s32[64]{0:T(128)S(1)} %collective-permute-done.4), kind=kOutput, calls=%fused_computation.76 | convolution fusion | flops 404234240 | bytes 10486272 | tf_op jit(solution)/shard_map/ts,tkc->ksc/dot_general | solution.py:54
  282.9 10.0 %fusion.311 = (bf16[64,8192]{1,0:T(8,128)(2,1)}, f32[64,8192]{1,0:T(8,128)}) fusion(f32[8,8,64,128]{3,2,1,0:T(8,128)S(1)} %bitcast.325, f32[8,8,64,128]{3,2,1,0:T(8,128)S(1)} %bitcast.323, f32[8,8,64,128]{3,2,1,0:T(8,128)S(1)} %bitcast.321, f32[8,8,64,128]{3,2,1,0:T(8,128)S(1)} %bitcast.318, bf16[64,8192]{1,0:T(8,128)(2,1)S(1)} %copy-done.8), kind=kLoop, calls=%fused_computation.374 | loop fusion | flops 8912896 | bytes 12582912 | tf_op jit(solution)/shard_map/convert_element_type | solution.py:110
  299.1 6.5 %collective-permute-start.13 = (bf16[64,8192]{1,0:T(8,128)(2,1)}, bf16[64,8192]{1,0:T(8,128)(2,1)}, u32[]{:S(2)}, u32[]{:S(2)}) collective-permute-start(bf16[64,8192]{1,0:T(8,128)(2,1)} %get-tuple-element.4), channel_id=1, source_target_pairs={{0,1},{1,2},{2,3},{3,4},{4,5},{5,6},{6,7},{7,8},{8,9},{9,10},{10,1... | collective-permute-start | bytes 3145736 | tf_op jit(solution)/shard_map/ppermute | solution.py:27
  305.6 4.1 fusion.313
  309.7 24.9 %all-gather = f32[256,64]{1,0:T(8,128)S(1)} all-gather(f32[64,64]{1,0:T(8,128)S(1)} %fusion.313), channel_id=2, replica_groups=mesh['grp_0'=4,'grp_1'=2,'row_0'=4,'row_1'=4] {'grp_0'}, dimensions={0}, use_global_device_ids=true | all-gather | bytes 81920 | tf_op jit(solution)/shard_map/all_gather | solution.py:41
  336.6 12.0 %all-gather.2 = f32[256,64]{1,0:T(8,128)S(1)} all-gather(f32[64,64]{1,0:T(8,128)S(1)} %reduce_sum.75), channel_id=4, replica_groups=mesh['grp_0'=4,'grp_1'=2,'row_0'=4,'row_1'=4] {'row_0'}, dimensions={0}, use_global_device_ids=true | all-gather | bytes 81920 | tf_op jit(solution)/shard_map/all_gather | solution.py:41
  348.6 14.2 %all-gather.3 = f32[256,64]{1,0:T(8,128)S(1)} all-gather(f32[64,64]{1,0:T(8,128)S(1)} %reduce_sum.76), channel_id=5, replica_groups=mesh['grp_0'=4,'grp_1'=2,'row_0'=4,'row_1'=4] {'row_1'}, dimensions={0}, use_global_device_ids=true | all-gather | bytes 81920 | tf_op jit(solution)/shard_map/all_gather | solution.py:41
  362.9 5.8 %cholesky.15 = f32[64,64]{1,0:T(8,128)S(1)} custom-call(f32[64,64]{1,0:T(8,128)S(1)} %fusion.165), custom_call_target="Cholesky" | custom-call | tf_op jit(solution)/shard_map/jit(cholesky)/cholesky | solution.py:121
  371.0 4.7 %fusion.14 = f32[64,128,64]{1,2,0:T(8,128)} fusion(f32[64,64,128]{2,1,0:T(8,128)S(1)} %fusion.65, f32[64]{0:T(128)S(1)} %compare_convert_fusion.2, s32[64]{0:T(128)S(1)} %copy-done.28), kind=kOutput, calls=%fused_computation.40 | convolution fusion | flops 402661376 | bytes 4194816 | tf_op jit(solution)/shard_map/ts,tkc->ksc/dot_general | solution.py:54
  376.3 4.9 %custom-call.10 = f32[1,64,64]{1,2,0:T(8,128)S(1)} custom-call(f32[1,64,64]{2,1,0:T(8,128)S(1)} %fusion.159), custom_call_target="InvertDiagBlocksLowerTriangular" | custom-call | tf_op jit(solution)/shard_map/jit(_solve_triangular)/triangular_solve | solution.py:122
  381.2 4.9 %fusion.163 = f32[64,8192]{1,0:T(8,128)} fusion(f32[64,8192]{1,0:T(8,128)} %get-tuple-element.5, f32[1,64,64]{1,2,0:T(8,128)S(1)} %custom-call.10), kind=kOutput, calls=%fused_computation.202 | convolution fusion | flops 402653184 | bytes 4210688 | tf_op jit(solution)/shard_map/jit(_solve_triangular)/triangular_solve | solution.py:122
  386.8 4.7 %fusion.12 = f32[64,128,64]{1,2,0:T(8,128)} fusion(f32[64,64,128]{2,1,0:T(8,128)S(1)} %fusion.63, s32[64]{0:T(128)S(1)} %copy-done.29, f32[64]{0:T(128)S(1)} %compare_convert_fusion.2), kind=kOutput, calls=%fused_computation.38 | convolution fusion | flops 402661376 | bytes 4194816 | tf_op jit(solution)/shard_map/ts,tkc->ksc/dot_general | solution.py:54
  394.9 3.5 fusion.61
  398.4 4.7 %fusion.10 = f32[64,128,64]{1,2,0:T(8,128)} fusion(f32[64,64,128]{2,1,0:T(8,128)S(1)} %fusion.61, f32[64]{0:T(128)S(1)} %compare_convert_fusion.1, s32[64]{0:T(128)S(1)} %copy-done.30), kind=kOutput, calls=%fused_computation.36 | convolution fusion | flops 402661376 | bytes 4194816 | tf_op jit(solution)/shard_map/ts,tkc->ksc/dot_general | solution.py:54
  406.2 2.8 fusion.59
  409.4 5.4 %add_add_fusion = f32[64,128,64]{1,2,0:T(8,128)S(1)} fusion(f32[64,128,64]{1,2,0:T(8,128)} %fusion.10, f32[64,128,64]{1,2,0:T(8,128)S(1)} %copy-done.13, f32[64,128,64]{1,2,0:T(8,128)S(1)} %copy-done.14, f32[64,64,128]{2,1,0:T(8,128)S(1)} %fusion.59, f32[64]{0:T(128)S(1)} %compare_convert_fusion, s32[64]{0:T(128)S(1)} %collective-permute-done.4), kind=kOutput, calls=%fused_computation.74 | convolution fusion | flops 404234240 | bytes 10486272 | tf_op jit(solution)/shard_map/ts,tkc->ksc/dot_general | solution.py:54
  414.8 4.3 fusion.1
  419.1 16.3 %all-gather.4 = f32[256,64]{1,0:T(8,128)S(1)} all-gather(f32[64,64]{1,0:T(8,128)S(1)} %fusion.1), channel_id=6, replica_groups=mesh['grp_0'=4,'grp_1'=2,'row_0'=4,'row_1'=4] {'grp_0'}, dimensions={0}, use_global_device_ids=true | all-gather | bytes 81920 | tf_op jit(solution)/shard_map/all_gather | solution.py:41
  437.3 12.0 %all-gather.6 = f32[256,64]{1,0:T(8,128)S(1)} all-gather(f32[64,64]{1,0:T(8,128)S(1)} %reduce_sum.80), channel_id=8, replica_groups=mesh['grp_0'=4,'grp_1'=2,'row_0'=4,'row_1'=4] {'row_0'}, dimensions={0}, use_global_device_ids=true | all-gather | bytes 81920 | tf_op jit(solution)/shard_map/all_gather | solution.py:41
  449.3 12.0 %all-gather.7 = f32[256,64]{1,0:T(8,128)S(1)} all-gather(f32[64,64]{1,0:T(8,128)S(1)} %reduce_sum.81), channel_id=9, replica_groups=mesh['grp_0'=4,'grp_1'=2,'row_0'=4,'row_1'=4] {'row_1'}, dimensions={0}, use_global_device_ids=true | all-gather | bytes 81920 | tf_op jit(solution)/shard_map/all_gather | solution.py:41
  (150 shorter events, 86.0 us)
Async XLA Ops:
  0.6 25.3 %copy-start = (bf16[64,128,128]{2,1,0:T(8,128)(2,1)S(1)}, bf16[64,128,128]{2,1,0:T(8,128)(2,1)}, u32[]{:S(2)}) copy-start(bf16[64,128,128]{2,1,0:T(8,128)(2,1)} %param.14) | copy-start | bytes 6291460
  0.6 21.3 %copy-start.29 = (s32[64]{0:T(128)S(1)}, s32[64]{0:T(128)}, u32[]{:S(2)}) copy-start(s32[64]{0:T(128)} %param.16) | copy-start | bytes 772
  0.7 21.3 %copy-start.28 = (s32[64]{0:T(128)S(1)}, s32[64]{0:T(128)}, u32[]{:S(2)}) copy-start(s32[64]{0:T(128)} %param.15) | copy-start | bytes 772
  0.7 78.3 %collective-permute-start = (bf16[64,8192]{1,0:T(8,128)(2,1)}, bf16[64,8192]{1,0:T(8,128)(2,1)}, u32[]{:S(2)}, u32[]{:S(2)}) collective-permute-start(bf16[64,8192]{1,0:T(8,128)(2,1)} %param.13), channel_id=1, source_target_pairs={{1,0},{2,1},{3,2},{4,3},{5,4},{6,5},{7,6},{8,7},{9,8},{10,9},{11,1... | collective-permute-start | bytes 3145736 | tf_op jit(solution)/shard_map/ppermute | solution.py:28
  2.1 80.1 %collective-permute-start.1 = (bf16[64,8192]{1,0:T(8,128)(2,1)}, bf16[64,8192]{1,0:T(8,128)(2,1)}, u32[]{:S(2)}, u32[]{:S(2)}) collective-permute-start(bf16[64,8192]{1,0:T(8,128)(2,1)} %param.13), channel_id=1, source_target_pairs={{0,1},{1,2},{2,3},{3,4},{4,5},{5,6},{6,7},{7,8},{8,9},{9,10},{10,1... | collective-permute-start | bytes 3145736 | tf_op jit(solution)/shard_map/ppermute | solution.py:27
  7.6 84.5 %collective-permute-start.3 = (bf16[64,128,128]{2,1,0:T(8,128)(2,1)}, bf16[64,128,128]{2,1,0:T(8,128)(2,1)}, u32[]{:S(2)}, u32[]{:S(2)}) collective-permute-start(bf16[64,128,128]{2,1,0:T(8,128)(2,1)} %param.18), channel_id=1, source_target_pairs={{0,1},{1,2},{2,3},{3,4},{4,5},{5,6},{6,7},{7,8},{8,9},{9,10},{10,1... | collective-permute-start | bytes 6291464 | tf_op jit(solution)/shard_map/ppermute | solution.py:16
  11.6 59.8 %collective-permute-start.5 = (s32[1]{0:T(128)}, s32[1]{0:T(128)}, u32[]{:S(2)}, u32[]{:S(2)}) collective-permute-start(s32[1]{0:T(128)} %param.21), channel_id=1, source_target_pairs={{0,1},{1,2},{2,3},{3,4},{4,5},{5,6},{6,7},{7,8},{8,9},{9,10},{10,1... | collective-permute-start | bytes 20 | tf_op jit(solution)/shard_map/ppermute | solution.py:16
  14.3 80.4 %collective-permute-start.4 = (s32[64]{0:T(128)}, s32[64]{0:T(128)S(1)}, u32[]{:S(2)}, u32[]{:S(2)}) collective-permute-start(s32[64]{0:T(128)} %param.20), channel_id=1, source_target_pairs={{0,1},{1,2},{2,3},{3,4},{4,5},{5,6},{6,7},{7,8},{8,9},{9,10},{10,1... | collective-permute-start | bytes 776 | tf_op jit(solution)/shard_map/ppermute | solution.py:16
  28.7 4.7 %copy-start.27 = (bf16[64,64,128]{2,1,0:T(8,128)(2,1)S(1)}, bf16[64,64,128]{2,1,0:T(8,128)(2,1)}, u32[]{:S(2)}) copy-start(bf16[64,64,128]{2,1,0:T(8,128)(2,1)} %gather_fusion.1) | copy-start | bytes 3145732
  34.1 4.7 %copy-start.31 = (s32[64]{0:T(128)S(1)}, s32[64]{0:T(128)}, u32[]{:S(2)}) copy-start(s32[64]{0:T(128)} %param.20) | copy-start | bytes 772
  34.1 37.3 %copy-start.30 = (s32[64]{0:T(128)S(1)}, s32[64]{0:T(128)}, u32[]{:S(2)}) copy-start(s32[64]{0:T(128)} %param.19) | copy-start | bytes 772
  71.4 7.5 %collective-permute-start.2 = (s32[64]{0:T(128)S(1)}, s32[64]{0:T(128)S(1)}, u32[]{:S(2)}, u32[]{:S(2)}) collective-permute-start(s32[64]{0:T(128)S(1)} %copy-done.30), channel_id=1, source_target_pairs={{0,1},{1,2},{2,3},{3,4},{4,5},{5,6},{6,7},{7,8},{8,9},{9,10},{10,1... | collective-permute-start | bytes 776 | tf_op jit(solution)/shard_map/ppermute | solution.py:16
  88.8 3.4 copy-start.26
  92.2 2.5 copy-start.11
  92.2 2.8 copy-start.12
  94.7 4.1 copy-start.8
  98.8 2.5 copy-start.1
  101.3 28.9 %collective-permute-start.6 = (bf16[64,8192]{1,0:T(8,128)(2,1)}, bf16[64,8192]{1,0:T(8,128)(2,1)}, u32[]{:S(2)}, u32[]{:S(2)}) collective-permute-start(bf16[64,8192]{1,0:T(8,128)(2,1)} %multiply_convert_fusion), channel_id=1, source_target_pairs={{1,0},{2,1},{3,2},{4,3},{5,4},{6,5},{7,6},{8,7},{9,8},{10,9},{11,1... | collective-permute-start | bytes 3145736 | tf_op jit(solution)/shard_map/ppermute | solution.py:28
  110.9 33.1 %collective-permute-start.7 = (bf16[64,8192]{1,0:T(8,128)(2,1)}, bf16[64,8192]{1,0:T(8,128)(2,1)}, u32[]{:S(2)}, u32[]{:S(2)}) collective-permute-start(bf16[64,8192]{1,0:T(8,128)(2,1)} %multiply_convert_fusion), channel_id=1, source_target_pairs={{0,1},{1,2},{2,3},{3,4},{4,5},{5,6},{6,7},{7,8},{8,9},{9,10},{10,1... | collective-permute-start | bytes 3145736 | tf_op jit(solution)/shard_map/ppermute | solution.py:27
  120.2 4.7 %copy-start.23 = (bf16[64,64,128]{2,1,0:T(8,128)(2,1)S(1)}, bf16[64,64,128]{2,1,0:T(8,128)(2,1)}, u32[]{:S(2)}) copy-start(bf16[64,64,128]{2,1,0:T(8,128)(2,1)} %gather_fusion.5) | copy-start | bytes 3145732
  149.5 2.8 copy-start.15
  149.5 3.2 copy-start.18
  152.7 5.6 %copy-start.2 = (f32[64,128,64]{1,2,0:T(8,128)S(1)}, f32[64,128,64]{1,2,0:T(8,128)}, u32[]{:S(2)}) copy-start(f32[64,128,64]{1,2,0:T(8,128)} %copy-done.1) | copy-start | bytes 6291460
  158.2 4.4 copy-start.5
  162.6 28.2 %collective-permute-start.8 = (bf16[64,8192]{1,0:T(8,128)(2,1)}, bf16[64,8192]{1,0:T(8,128)(2,1)}, u32[]{:S(2)}, u32[]{:S(2)}) collective-permute-start(bf16[64,8192]{1,0:T(8,128)(2,1)} %fusion.310), channel_id=1, source_target_pairs={{1,0},{2,1},{3,2},{4,3},{5,4},{6,5},{7,6},{8,7},{9,8},{10,9},{11,1... | collective-permute-start | bytes 3145736 | tf_op jit(solution)/shard_map/ppermute | solution.py:28
  172.2 32.7 %collective-permute-start.9 = (bf16[64,8192]{1,0:T(8,128)(2,1)}, bf16[64,8192]{1,0:T(8,128)(2,1)}, u32[]{:S(2)}, u32[]{:S(2)}) collective-permute-start(bf16[64,8192]{1,0:T(8,128)(2,1)} %fusion.310), channel_id=1, source_target_pairs={{0,1},{1,2},{2,3},{3,4},{4,5},{5,6},{6,7},{7,8},{8,9},{9,10},{10,1... | collective-permute-start | bytes 3145736 | tf_op jit(solution)/shard_map/ppermute | solution.py:27
  180.7 4.7 %copy-start.24 = (bf16[64,64,128]{2,1,0:T(8,128)(2,1)S(1)}, bf16[64,64,128]{2,1,0:T(8,128)(2,1)}, u32[]{:S(2)}) copy-start(bf16[64,64,128]{2,1,0:T(8,128)(2,1)} %gather_fusion.9) | copy-start | bytes 3145732
  210.3 2.8 copy-start.16
  210.3 3.2 copy-start.19
  213.4 5.5 %copy-start.3 = (f32[64,128,64]{1,2,0:T(8,128)S(1)}, f32[64,128,64]{1,2,0:T(8,128)}, u32[]{:S(2)}) copy-start(f32[64,128,64]{1,2,0:T(8,128)} %copy-done.1) | copy-start | bytes 6291460
  213.4 5.5 %copy-start.6 = (f32[64,128,64]{1,2,0:T(8,128)S(1)}, f32[64,128,64]{1,2,0:T(8,128)}, u32[]{:S(2)}) copy-start(f32[64,128,64]{1,2,0:T(8,128)} %copy-done.5) | copy-start | bytes 6291460
  219.0 6.1 %copy-start.9 = (f32[64,128,64]{1,2,0:T(8,128)}, f32[64,128,64]{1,2,0:T(8,128)S(1)}, u32[]{:S(2)}) copy-start(f32[64,128,64]{1,2,0:T(8,128)S(1)} %add_add_fusion.2) | copy-start | bytes 6291460
  225.1 29.8 %collective-permute-start.10 = (bf16[64,8192]{1,0:T(8,128)(2,1)}, bf16[64,8192]{1,0:T(8,128)(2,1)}, u32[]{:S(2)}, u32[]{:S(2)}) collective-permute-start(bf16[64,8192]{1,0:T(8,128)(2,1)} %fusion.309), channel_id=1, source_target_pairs={{1,0},{2,1},{3,2},{4,3},{5,4},{6,5},{7,6},{8,7},{9,8},{10,9},{11,1... | collective-permute-start | bytes 3145736 | tf_op jit(solution)/shard_map/ppermute | solution.py:28
  234.7 34.1 %collective-permute-start.11 = (bf16[64,8192]{1,0:T(8,128)(2,1)}, bf16[64,8192]{1,0:T(8,128)(2,1)}, u32[]{:S(2)}, u32[]{:S(2)}) collective-permute-start(bf16[64,8192]{1,0:T(8,128)(2,1)} %fusion.309), channel_id=1, source_target_pairs={{0,1},{1,2},{2,3},{3,4},{4,5},{5,6},{6,7},{7,8},{8,9},{9,10},{10,1... | collective-permute-start | bytes 3145736 | tf_op jit(solution)/shard_map/ppermute | solution.py:27
  244.7 4.7 %copy-start.25 = (bf16[64,64,128]{2,1,0:T(8,128)(2,1)S(1)}, bf16[64,64,128]{2,1,0:T(8,128)(2,1)}, u32[]{:S(2)}) copy-start(bf16[64,64,128]{2,1,0:T(8,128)(2,1)} %gather_fusion.13) | copy-start | bytes 3145732
  274.2 2.8 copy-start.17
  274.2 3.2 copy-start.20
  277.4 5.5 %copy-start.4 = (f32[64,128,64]{1,2,0:T(8,128)S(1)}, f32[64,128,64]{1,2,0:T(8,128)}, u32[]{:S(2)}) copy-start(f32[64,128,64]{1,2,0:T(8,128)} %copy-done.1) | copy-start | bytes 6291460
  277.4 5.5 %copy-start.7 = (f32[64,128,64]{1,2,0:T(8,128)S(1)}, f32[64,128,64]{1,2,0:T(8,128)}, u32[]{:S(2)}) copy-start(f32[64,128,64]{1,2,0:T(8,128)} %copy-done.5) | copy-start | bytes 6291460
  277.4 5.5 %copy-start.10 = (f32[64,128,64]{1,2,0:T(8,128)S(1)}, f32[64,128,64]{1,2,0:T(8,128)}, u32[]{:S(2)}) copy-start(f32[64,128,64]{1,2,0:T(8,128)} %copy-done.9) | copy-start | bytes 6291460
  292.9 98.6 %collective-permute-start.12 = (bf16[64,8192]{1,0:T(8,128)(2,1)}, bf16[64,8192]{1,0:T(8,128)(2,1)}, u32[]{:S(2)}, u32[]{:S(2)}) collective-permute-start(bf16[64,8192]{1,0:T(8,128)(2,1)} %get-tuple-element.4), channel_id=1, source_target_pairs={{1,0},{2,1},{3,2},{4,3},{5,4},{6,5},{7,6},{8,7},{9,8},{10,9},{11,1... | collective-permute-start | bytes 3145736 | tf_op jit(solution)/shard_map/ppermute | solution.py:28
  299.1 104.0 %collective-permute-start.13 = (bf16[64,8192]{1,0:T(8,128)(2,1)}, bf16[64,8192]{1,0:T(8,128)(2,1)}, u32[]{:S(2)}, u32[]{:S(2)}) collective-permute-start(bf16[64,8192]{1,0:T(8,128)(2,1)} %get-tuple-element.4), channel_id=1, source_target_pairs={{0,1},{1,2},{2,3},{3,4},{4,5},{5,6},{6,7},{7,8},{8,9},{9,10},{10,1... | collective-permute-start | bytes 3145736 | tf_op jit(solution)/shard_map/ppermute | solution.py:27
  305.6 63.8 %copy-start.22 = (bf16[64,64,128]{2,1,0:T(8,128)(2,1)S(1)}, bf16[64,64,128]{2,1,0:T(8,128)(2,1)}, u32[]{:S(2)}) copy-start(bf16[64,64,128]{2,1,0:T(8,128)(2,1)} %gather_fusion.16) | copy-start | bytes 3145732
  381.2 4.9 %copy-start.21 = (bf16[64,64,128]{2,1,0:T(8,128)(2,1)S(1)}, bf16[64,64,128]{2,1,0:T(8,128)(2,1)}, u32[]{:S(2)}) copy-start(bf16[64,64,128]{2,1,0:T(8,128)(2,1)} %gather_fusion.17) | copy-start | bytes 3145732
  406.2 2.8 copy-start.13
  406.2 3.2 copy-start.14
